TPU v7x, 32 devices: a whole 2x2x4 slice. The times are simulated.
32 devices in a mesh: seq: 16 (over z, y, x), rep: 2 (over core).
Axes of the slice: x: 2, y: 2, z: 4, core: 2. Of those that a mesh axis runs over, the one named last changes fastest.
Arguments:
- tokens: bfloat16 [4, 48, 180, 768], P('rep', 'seq'), may hold values from -6 to 6
- cotangent: bfloat16 [4, 48, 180, 768], P('rep', 'seq'), may hold values from -6 to 6
- in_weight: bfloat16 [2, 8, 96, 96], replicated, may hold values from -0.21875 to 0.21875
- in_bias: float32 [2, 768], replicated, may hold values from -0.6 to 0.6
- out_weight: bfloat16 [2, 8, 96, 96], replicated, may hold values from -0.21875 to 0.21875
- out_bias: float32 [2, 768], replicated, may hold values from -0.12 to 0.12
Outputs:
- mixed_out: bfloat16 [4, 48, 180, 768], P('rep', 'seq')
- tokens_grad: bfloat16 [4, 48, 180, 768], P('rep', 'seq')
- in_weight_grad: float32 [2, 8, 96, 96], replicated
- in_bias_grad: float32 [2, 768], replicated
- out_weight_grad: float32 [2, 8, 96, 96], replicated
- out_bias_grad: float32 [2, 768], replicated
All inputs are finite; a program needn't handle non-finite values.
Results may differ from a plain program's by a relative error of at most 0.0094.
Values may be sent and summed in bfloat16 or wider, within the bound.
A program may use at most 64 MiB of HBM per device.

v0:
```python
import functools
import math

import jax
import jax.numpy as jnp
import ml_dtypes
import numpy as np
from jax import lax
from jax.experimental import pallas as pl
from jax.experimental.pallas import tpu as pltpu
from jax.sharding import PartitionSpec as P

BLOCKS = 8
BLOCK = 96
MODES = 64


def grid_tables(length, modes):
    position = jnp.arange(length, dtype=jnp.int32)
    frequency = jnp.arange(modes, dtype=jnp.int32)
    residue = position[:, None] * frequency[None, :] % length
    angles = residue.astype(jnp.float32) * (2.0 * math.pi / length)
    factor = 1.0 / math.sqrt(length)
    cosine_table = (jnp.cos(angles) * factor).astype(jnp.bfloat16)
    sine_table = (jnp.sin(angles) * factor).astype(jnp.bfloat16)
    return (cosine_table, sine_table)


def column_tables(grid_width, modes):
    cosine_table, sine_table = grid_tables(grid_width, modes)
    forward = jnp.stack([cosine_table, -sine_table], axis=2)
    doubling = jnp.where(jnp.arange(modes) == 0, 1.0, 2.0).astype(jnp.bfloat16)[:, None]
    inverse = jnp.stack([cosine_table.T * doubling, -(sine_table.T * doubling)], axis=1)
    return (forward, inverse)


def row_table(length):
    cosine_table, sine_table = grid_tables(length, length)
    upper_rows = jnp.stack([cosine_table, sine_table], axis=2)
    lower_rows = jnp.stack([-sine_table, cosine_table], axis=2)
    return jnp.stack([upper_rows, lower_rows], axis=1)


def block_weights(weight):
    real_part, imag_part = (weight[0], weight[1])
    upper_half = jnp.stack([real_part, imag_part], axis=2)
    lower_half = jnp.stack([-imag_part, real_part], axis=2)
    return jnp.stack([upper_half, lower_half], axis=1)


def fold_blocks(blockwise):
    real_part = blockwise[:, 0, :, 0, :] + blockwise[:, 1, :, 1, :]
    imag_part = blockwise[:, 0, :, 1, :] - blockwise[:, 1, :, 0, :]
    return jnp.stack([real_part, imag_part])


def mix_forward(spectrum, weights_in, weights_out, bias_in, bias_out):
    mode_count = spectrum.shape[0] * spectrum.shape[1] * spectrum.shape[2]
    flat_modes = spectrum.reshape(mode_count, 2, BLOCKS, BLOCK)
    hidden_pre = (
        jnp.einsum("mcbi,bciej->mebj", flat_modes, weights_in, preferred_element_type=jnp.float32)
        + bias_in
    )
    hidden = jax.nn.gelu(hidden_pre).astype(jnp.bfloat16)
    spectrum_out = (
        jnp.einsum("mcbi,bciej->mebj", hidden, weights_out, preferred_element_type=jnp.float32)
        + bias_out
    )
    return (
        flat_modes,
        hidden_pre,
        hidden,
        spectrum_out.astype(jnp.bfloat16).reshape(spectrum.shape),
    )


def mix_backward(flat_modes, hidden_pre, hidden, incoming, weights_in, weights_out):
    incoming_flat = incoming.reshape(flat_modes.shape)
    out_bias_part = jnp.sum(incoming_flat.astype(jnp.float32), axis=0).reshape(2, -1)
    out_weight_part = fold_blocks(
        jnp.einsum("mcbi,mebj->bciej", hidden, incoming_flat, preferred_element_type=jnp.float32)
    )
    hidden_grad = jnp.einsum(
        "mebj,bciej->mcbi", incoming_flat, weights_out, preferred_element_type=jnp.float32
    )
    pre_grad = jax.vjp(jax.nn.gelu, hidden_pre)[1](hidden_grad)[0].astype(jnp.bfloat16)
    in_bias_part = jnp.sum(pre_grad.astype(jnp.float32), axis=0).reshape(2, -1)
    in_weight_part = fold_blocks(
        jnp.einsum("mcbi,mebj->bciej", flat_modes, pre_grad, preferred_element_type=jnp.float32)
    )
    spectrum_grad = jnp.einsum(
        "mebj,bciej->mcbi", pre_grad, weights_in, preferred_element_type=jnp.float32
    )
    spectrum_grad = spectrum_grad.astype(jnp.bfloat16).reshape(incoming.shape)
    return (spectrum_grad, (in_weight_part, in_bias_part, out_weight_part, out_bias_part))


def shards_plain(tokens, cotangent, in_weight, in_bias, out_weight, out_bias):
    samples, row_count, grid_width, channels = tokens.shape
    length = row_count * lax.axis_size("seq")
    column_forward, column_inverse = column_tables(grid_width, MODES)
    row_matrix = row_table(length)
    weights_in = block_weights(in_weight)
    weights_out = block_weights(out_weight)
    bias_in = in_bias.reshape(2, BLOCKS, BLOCK)
    bias_out = out_bias.reshape(2, BLOCKS, BLOCK)

    def along_rows(section):
        return jnp.einsum(
            "qehc,shkcd->sqked", row_matrix, section, preferred_element_type=jnp.float32
        ).astype(jnp.bfloat16)

    def back_rows(section):
        return jnp.einsum(
            "qehc,sqked->shkcd", row_matrix, section, preferred_element_type=jnp.float32
        ).astype(jnp.bfloat16)

    spec_rows = jnp.einsum(
        "shwd,wkc->shkcd", tokens, column_forward, preferred_element_type=jnp.float32
    ).astype(jnp.bfloat16)
    spectrum = along_rows(lax.all_to_all(spec_rows, "seq", split_axis=2, concat_axis=1, tiled=True))
    flat_modes, hidden_pre, hidden, spectrum_out = mix_forward(
        spectrum, weights_in, weights_out, bias_in, bias_out
    )
    mixed_grid = jnp.einsum(
        "shkcd,kcw->shwd",
        lax.all_to_all(back_rows(spectrum_out), "seq", split_axis=1, concat_axis=2, tiled=True),
        column_inverse,
        preferred_element_type=jnp.float32,
    )
    cot_rows = jnp.einsum(
        "shwd,kcw->shkcd", cotangent, column_inverse, preferred_element_type=jnp.float32
    ).astype(jnp.bfloat16)
    incoming = along_rows(lax.all_to_all(cot_rows, "seq", split_axis=2, concat_axis=1, tiled=True))
    spectrum_grad, partials = mix_backward(
        flat_modes, hidden_pre, hidden, incoming, weights_in, weights_out
    )
    adjoint_part = jnp.einsum(
        "shkcd,wkc->shwd",
        lax.all_to_all(back_rows(spectrum_grad), "seq", split_axis=1, concat_axis=2, tiled=True),
        column_forward,
        preferred_element_type=jnp.float32,
    )
    mixed_out = (tokens.astype(jnp.float32) + mixed_grid).astype(jnp.bfloat16)
    tokens_grad = (cotangent.astype(jnp.float32) + adjoint_part).astype(jnp.bfloat16)
    totals = lax.psum((partials[0], partials[1], partials[2], partials[3]), ("seq", "rep"))
    divisor = float(samples * lax.axis_size("rep"))
    return (
        mixed_out,
        tokens_grad,
        totals[0] / divisor,
        totals[1] / divisor,
        totals[2] / divisor,
        totals[3] / divisor,
    )


GROUP = math.lcm(BLOCK, 128)
PER_GROUP = GROUP // BLOCK
COPY_A, COPY_B, COPY_C, COPY_E, COPY_F, COPY_G, COPY_H, COPY_D = range(8)
MESH_ID = pl.DeviceIdType.MESH


def host_tables(length, modes):
    residue = np.arange(length)[:, None] * np.arange(modes)[None, :] % length
    angles = residue.astype(np.float32) * np.float32(2.0 * math.pi / length)
    factor = np.float32(1.0 / math.sqrt(length))
    rounded = [(f(angles) * factor).astype(ml_dtypes.bfloat16) for f in (np.cos, np.sin)]
    return [table.astype(np.float32) for table in rounded]


def kernel_tables(width, length, n, samples, rows):
    local = MODES // n
    cosine, sine = host_tables(width, MODES)
    forward = np.stack([cosine.T, -sine.T], axis=1)
    doubled = forward * np.where(np.arange(MODES) == 0, 1.0, 2.0)[:, None, None]

    def spread(table):
        table = table.reshape(n, local, 2, width)
        whole = np.zeros((n, samples, local, 2, width, samples), np.float32)
        for s in range(samples):
            whole[:, s, :, :, :, s] = table
        return whole.reshape(n * samples * local * 2, width * samples)

    cosine, sine = host_tables(length, length)
    upper = np.stack([cosine, sine], axis=2)
    lower = np.stack([-sine, cosine], axis=2)
    turn = np.stack([upper, lower], axis=0)
    both = samples * local
    mixing = np.zeros((2, both, length, length, both, 2), np.float32)
    for x in range(both):
        mixing[:, x, :, :, x, :] = turn
    mixing = mixing.reshape(2 * both * length, length * both * 2)

    flat = [
        spread(forward),
        spread(doubled),
        spread(doubled).T,
        spread(forward).T,
        mixing,
    ]
    return [np.ascontiguousarray(t).astype(ml_dtypes.bfloat16) for t in flat]


def dot(a, b, contract=(1, 0)):
    return lax.dot_general(
        a, b, (((contract[0],), (contract[1],)), ((), ())), preferred_element_type=jnp.float32
    )


def mixer(
    n,
    inner,
    divisor,
    tok,
    cot,
    col_tok,
    col_cot,
    inv_mix,
    inv_grad,
    turn,
    in_weight,
    in_bias,
    out_weight,
    out_bias,
    mixed,
    grad,
    in_weight_grad,
    in_bias_grad,
    out_weight_grad,
    out_bias_grad,
    send_a,
    send_b,
    send_c,
    send_d,
    send_e,
    send_f,
    recv_a,
    recv_b,
    recv_c,
    recv_d,
    recv_e,
    recv_f,
    turn_back,
    wide,
    spec,
    hid,
    slope,
    inc,
    pre,
    mixed_modes,
    grads,
    halves,
    half_in,
    part,
    gathered,
    other,
    both,
    send_sem,
    recv_sem,
    pair_send,
    pair_recv,
):
    me = lax.axis_index("seq")
    core = lax.axis_index("rep")
    partner = 1 - core
    rows, width, samples, channels = tok.shape
    groups = channels // GROUP
    outer = n // inner
    across, within = me // inner, lax.rem(me, inner)
    chunk = send_a.shape[1]
    row_chunk = chunk // rows
    bf16 = jnp.bfloat16

    barrier = pltpu.get_barrier_semaphore()

    def greet(j, carry):
        peer = lax.rem(me + j, n)
        pl.semaphore_signal(barrier, inc=1, device_id={"seq": peer}, device_id_type=MESH_ID)
        return carry

    lax.fori_loop(1, n, greet, 0)
    pl.semaphore_signal(barrier, inc=1, device_id={"rep": partner}, device_id_type=MESH_ID)

    def copy_to(phase, peer, mine, source, target):
        return pltpu.make_async_remote_copy(
            src_ref=source,
            dst_ref=target,
            send_sem=send_sem.at[phase, peer],
            recv_sem=recv_sem.at[phase, mine],
            device_id={"seq": peer},
            device_id_type=MESH_ID,
        )

    def loop(count, act):
        def step(j, carry):
            act(j)
            return carry

        lax.fori_loop(1, count, step, 0)

    def peer_at(j):
        return lax.rem(me + j, n)

    def plane_at(j):
        return lax.rem(within + j, inner)

    def line_at(j):
        return lax.rem(across + j, outer)

    def everyone(phase, source, target, at=None):
        cut = (lambda ref, i: ref.at[i]) if at is None else (lambda ref, i: ref.at[i, at])

        def out(j):
            peer = peer_at(j)
            return copy_to(phase, peer, me, cut(source, peer), cut(target, me))

        def back(j):
            peer = peer_at(j)
            return copy_to(phase, peer, peer, cut(source, peer), cut(target, peer))

        return (
            lambda: loop(n, lambda j: out(j).start()),
            lambda: loop(n, lambda j: back(j).wait_recv()),
            lambda: loop(n, lambda j: out(j).wait_send()),
        )

    def plane(phase, source, target):
        def out(j):
            v = plane_at(j)
            peer = across * inner + v
            return copy_to(phase, peer, me, source(v), target(within))

        def back(j):
            v = plane_at(j)
            peer = across * inner + v
            return copy_to(phase, peer, peer, source(v), target(v))

        return (
            lambda: loop(inner, lambda j: out(j).start()),
            lambda: loop(inner, lambda j: back(j).wait_recv()),
            lambda: loop(inner, lambda j: out(j).wait_send()),
        )

    def line(phase, source, target):
        def out(j):
            z = line_at(j)
            peer = z * inner + within
            return copy_to(phase, peer, me, source(z), target(across))

        def back(j):
            z = line_at(j)
            peer = z * inner + within
            return copy_to(phase, peer, peer, source(z), target(z))

        return (
            lambda: loop(outer, lambda j: out(j).start()),
            lambda: loop(outer, lambda j: back(j).wait_recv()),
            lambda: loop(outer, lambda j: out(j).wait_send()),
        )

    move_a = everyone(COPY_A, send_a, recv_a)
    move_b = everyone(COPY_B, send_b, recv_b)
    move_c = everyone(COPY_C, send_c, recv_c)
    pieces = [
        everyone(COPY_D + h, send_d, recv_d, pl.ds(h * row_chunk, row_chunk))
        for h in range(rows)
    ]
    move_e = plane(COPY_E, lambda v: send_e.at[v], lambda v: recv_e.at[v])
    move_f = line(COPY_F, lambda z: send_f.at[z], lambda z: recv_f.at[z])
    move_g = line(COPY_G, lambda z: part, lambda z: gathered.at[within, z])
    move_h = plane(COPY_H, lambda v: gathered.at[within], lambda v: gathered.at[v])

    def columns(tokens, table, send):
        for h in range(rows):
            product = dot(table[...], tokens[h].reshape(width * samples, channels))
            send[:, h * row_chunk : (h + 1) * row_chunk, :] = product.astype(bf16).reshape(
                n, row_chunk, channels
            )

    columns(tok, col_tok, send_a)
    pl.semaphore_wait(barrier, n)
    move_a[0]()
    columns(cot, col_cot, send_b)
    move_b[0]()
    recv_a[me] = send_a[me]
    recv_b[me] = send_b[me]

    turn_back[...] = turn[...].T
    row_at = lax.broadcasted_iota(jnp.int32, (BLOCK, GROUP), 0)
    lane_at = lax.broadcasted_iota(jnp.int32, (BLOCK, GROUP), 1)
    for at, weight in enumerate((in_weight, out_weight)):
        for i in range(PER_GROUP):
            place = (lane_at == row_at + i * BLOCK).astype(bf16)
            for c in range(2):
                for g in range(groups):
                    wide[2 * at + c, g, i * BLOCK : (i + 1) * BLOCK, :] = dot(
                        weight[c, g * PER_GROUP + i], place
                    ).astype(bf16)

    half = turn.shape[0] // 2
    scale = math.sqrt(2.0 / math.pi)

    def lanes(g):
        return pl.ds(pl.multiple_of(g * GROUP, GROUP), GROUP)

    def per_group(act):
        def step(g, carry):
            act(g, lanes(g))
            return carry

        lax.fori_loop(0, groups, step, 0)

    def along_rows(recv, at, keep, g):
        keep[g] = dot(turn[...], recv[:, :, at].reshape(turn.shape[1], GROUP)).astype(bf16)

    def back_rows(send, at):
        send[:, :, at] = (
            dot(turn_back[...], mixed_modes[...]).astype(bf16).reshape(n, chunk, GROUP)
        )

    def forward_group(g, at):
        along_rows(recv_a, at, spec, g)
        re, im = spec[g, :half], spec[g, half:]
        w_re, w_im = wide[0, g], wide[1, g]
        for c in range(2):
            if c == 0:
                value = dot(re, w_re) - dot(im, w_im)
            else:
                value = dot(re, w_im) + dot(im, w_re)
            value = value + in_bias[c : c + 1, at]
            square = value * value
            tanh = jnp.tanh(scale * value * (1.0 + 0.044715 * square))
            hid[g, c * half : (c + 1) * half] = (0.5 * value * (1.0 + tanh)).astype(bf16)
            slope[g, c * half : (c + 1) * half] = 0.5 * (1.0 + tanh) + 0.5 * value * (
                1.0 - tanh * tanh
            ) * (scale * (1.0 + (3.0 * 0.044715) * square))
        re, im = hid[g, :half], hid[g, half:]
        w_re, w_im = wide[2, g], wide[3, g]
        mixed_modes[:half] = (
            dot(re, w_re) - dot(im, w_im) + out_bias[0:1, at]
        ).astype(bf16)
        mixed_modes[half:] = (
            dot(re, w_im) + dot(im, w_re) + out_bias[1:2, at]
        ).astype(bf16)
        back_rows(send_c, at)

    move_a[1]()
    per_group(forward_group)
    move_c[0]()
    recv_c[me] = send_c[me]

    def backward_group(g, at):
        along_rows(recv_b, at, inc, g)
        re, im = inc[g, :half], inc[g, half:]
        w_re, w_im = wide[2, g], wide[3, g]
        pre[g, :half] = (
            (dot(re, w_re, (1, 1)) + dot(im, w_im, (1, 1))) * slope[g, :half]
        ).astype(bf16)
        pre[g, half:] = (
            (dot(im, w_re, (1, 1)) - dot(re, w_im, (1, 1))) * slope[g, half:]
        ).astype(bf16)
        re, im = pre[g, :half], pre[g, half:]
        w_re, w_im = wide[0, g], wide[1, g]
        mixed_modes[:half] = (dot(re, w_re, (1, 1)) + dot(im, w_im, (1, 1))).astype(bf16)
        mixed_modes[half:] = (dot(im, w_re, (1, 1)) - dot(re, w_im, (1, 1))).astype(bf16)
        back_rows(send_d, at)

    move_b[1]()
    per_group(backward_group)

    def fold(product):
        total = jnp.zeros((BLOCK, GROUP), jnp.float32)
        for i in range(PER_GROUP):
            inside = (lane_at >= i * BLOCK) & (lane_at < (i + 1) * BLOCK)
            total = jnp.where(inside, product[i * BLOCK : (i + 1) * BLOCK], total)
        return total.astype(bf16)

    bias_at = lax.broadcasted_iota(jnp.int32, (16, GROUP), 0)

    def grads_group(g, at):
        bias = jnp.zeros((16, GROUP), jnp.float32)
        for k, (left, right) in enumerate(((spec, pre), (hid, inc))):
            a_re, a_im = left[g, :half], left[g, half:]
            b_re, b_im = right[g, :half], right[g, half:]
            first = 2 * k * BLOCK
            grads[first : first + BLOCK, at] = fold(
                dot(a_re, b_re, (0, 0)) + dot(a_im, b_im, (0, 0))
            )
            grads[first + BLOCK : first + 2 * BLOCK, at] = fold(
                dot(a_re, b_im, (0, 0)) - dot(a_im, b_re, (0, 0))
            )
            for c, value in enumerate((b_re, b_im)):
                total = jnp.sum(value.astype(jnp.float32), axis=0, keepdims=True)
                bias = jnp.where(bias_at == 2 * k + c, total, bias)
        grads[4 * BLOCK : 4 * BLOCK + 16, at] = bias.astype(bf16)

    per_group(grads_group)
    per = 4 * BLOCK // (2 * n)
    to_row = lax.broadcasted_iota(jnp.int32, (2 * n * 16, 4 * BLOCK + 16), 0)
    from_row = lax.broadcasted_iota(jnp.int32, (2 * n * 16, 4 * BLOCK + 16), 1)
    slot = to_row % 16
    wanted = jnp.where(slot < per, to_row // 16 * per + slot, 4 * BLOCK + slot - per)
    picks = (wanted == from_row).astype(bf16)
    halves[...] = dot(picks, grads[...]).astype(bf16).reshape(halves.shape)

    def swap(slot, source, target):
        return pltpu.make_async_remote_copy(
            src_ref=source,
            dst_ref=target,
            send_sem=pair_send.at[slot],
            recv_sem=pair_recv.at[slot],
            device_id={"rep": partner},
            device_id_type=MESH_ID,
        )

    first_swap = swap(0, halves.at[partner], half_in)
    first_swap.start()

    def inverse_row(h, tokens, table, recv, out):
        section = recv[:, h * row_chunk : (h + 1) * row_chunk, :]
        product = dot(table[...], section.reshape(n * row_chunk, channels))
        kept = tokens[h].reshape(width * samples, channels).astype(jnp.float32)
        out[h] = (kept + product).astype(bf16).reshape(width, samples, channels)

    def inverse(tokens, table, recv, out):
        for h in range(rows):
            inverse_row(h, tokens, table, recv, out)

    first_swap.wait()
    send_e[...] = (
        (halves[core].astype(jnp.float32) + half_in[...].astype(jnp.float32))
        .astype(bf16)
        .reshape(send_e.shape)
    )
    move_e[0]()
    recv_e[within] = send_e[within]
    pieces[0][0]()
    recv_d[me] = send_d[me]
    move_c[1]()
    inverse(tok, inv_mix, recv_c, mixed)

    move_e[1]()
    send_f[...] = jnp.sum(recv_e[...].astype(jnp.float32), axis=0).astype(bf16)
    move_f[0]()
    recv_f[across] = send_f[across]
    middle = max(2, rows - 1)
    for piece in pieces[1:middle]:
        piece[0]()
    move_f[1]()
    total = jnp.sum(recv_f[...].astype(jnp.float32), axis=0) * (1.0 / divisor)
    in_bias_grad[...] = total[per : per + 2]
    out_bias_grad[...] = total[per + 2 : per + 4]
    part[...] = total.astype(bf16)
    move_g[0]()
    gathered[within, across] = part[...]
    for piece in pieces[middle:]:
        piece[0]()
    pieces[0][1]()
    inverse_row(0, cot, inv_grad, recv_d, grad)
    move_g[1]()
    move_h[0]()
    for h in range(1, rows - 1):
        pieces[h][1]()
        inverse_row(h, cot, inv_grad, recv_d, grad)
    move_h[1]()
    last_swap = swap(1, gathered, other)
    last_swap.start()
    both[core] = gathered[...].reshape(n * 16, channels)
    for h in range(max(1, rows - 1), rows):
        pieces[h][1]()
        inverse_row(h, cot, inv_grad, recv_d, grad)
    last_swap.wait()
    both[partner] = other[...].reshape(n * 16, channels)
    to_row = lax.broadcasted_iota(jnp.int32, (2 * BLOCK, n * 16), 0)
    from_row = lax.broadcasted_iota(jnp.int32, (2 * BLOCK, n * 16), 1)
    order = (to_row // per * 16 + to_row % per == from_row).astype(bf16)
    for k, out in enumerate((in_weight_grad, out_weight_grad)):
        for g in range(groups):
            ordered = dot(order, both[k, :, g * GROUP : (g + 1) * GROUP]).astype(bf16)
            for i in range(PER_GROUP):
                place = (lane_at == row_at + i * BLOCK).astype(bf16)
                block = dot(ordered, place, (1, 1))
                for c in range(2):
                    out[c, g * PER_GROUP + i] = block[c * BLOCK : (c + 1) * BLOCK]

    for move in (move_a, move_b, move_c, move_e, move_f, move_g, move_h, *pieces):
        move[2]()


def fits(n, reps, samples, rows, channels):
    per_row = samples * (MODES // n) * 2
    return (
        reps == 2
        and MODES % n == 0
        and per_row % 16 == 0
        and channels % GROUP == 0
        and channels == BLOCKS * BLOCK
        and (4 * BLOCK) % (2 * n) == 0
        and n > 1
        and n & (n - 1) == 0
        and rows > 1
        and 4 * BLOCK // (2 * n) + 4 <= 16
        and (samples * MODES // n * rows * n) % 16 == 0
    )


def shards(tokens, cotangent, in_weight, in_bias, out_weight, out_bias):
    samples, rows, width, channels = tokens.shape
    n, reps = lax.axis_size("seq"), lax.axis_size("rep")
    if not fits(n, reps, samples, rows, channels):
        return shards_plain(tokens, cotangent, in_weight, in_bias, out_weight, out_bias)
    length = rows * n
    inner = 2 ** ((n.bit_length() - 1) // 2)
    outer = n // inner
    chunk = rows * samples * (MODES // n) * 2
    whole = n * chunk
    groups = channels // GROUP
    tables = [jnp.asarray(t) for t in kernel_tables(width, length, n, samples, rows)]
    bf16, f32 = jnp.bfloat16, jnp.float32
    block = pltpu.VMEM((n, chunk, channels), bf16)
    small = pltpu.VMEM((n, 16, channels), bf16)
    ringed = pltpu.VMEM((inner, outer, 16, channels), bf16)
    lined = pltpu.VMEM((outer, 16, channels), bf16)
    planes = (tokens.transpose(1, 2, 0, 3), cotangent.transpose(1, 2, 0, 3))
    kept = pltpu.VMEM((groups, whole, GROUP), bf16)
    vmem = pl.BlockSpec(memory_space=pltpu.VMEM)
    mixed, grad, *parameter_grads = pl.pallas_call(
        functools.partial(mixer, n, inner, float(samples * reps)),
        out_shape=(
            jax.ShapeDtypeStruct(planes[0].shape, bf16),
            jax.ShapeDtypeStruct(planes[1].shape, bf16),
            jax.ShapeDtypeStruct(in_weight.shape, f32),
            jax.ShapeDtypeStruct(in_bias.shape, f32),
            jax.ShapeDtypeStruct(out_weight.shape, f32),
            jax.ShapeDtypeStruct(out_bias.shape, f32),
        ),
        in_specs=[vmem] * 11,
        out_specs=(vmem,) * 6,
        scratch_shapes=[block] * 4
        + [ringed, lined]
        + [block] * 4
        + [ringed, lined]
        + [
            pltpu.VMEM((whole, whole), bf16),
            pltpu.VMEM((4, groups, GROUP, GROUP), bf16),
            kept,
            kept,
            pltpu.VMEM((groups, whole, GROUP), f32),
            kept,
            kept,
            pltpu.VMEM((whole, GROUP), bf16),
            pltpu.VMEM((4 * BLOCK + 16, channels), bf16),
            pltpu.VMEM((2, n, 16, channels), bf16),
            small,
            pltpu.VMEM((16, channels), bf16),
            ringed,
            ringed,
            pltpu.VMEM((2, n * 16, channels), bf16),
            pltpu.SemaphoreType.DMA((COPY_D + rows, n)),
            pltpu.SemaphoreType.DMA((COPY_D + rows, n)),
            pltpu.SemaphoreType.DMA((2,)),
            pltpu.SemaphoreType.DMA((2,)),
        ],
        compiler_params=pltpu.CompilerParams(
            collective_id=0, has_side_effects=True, vmem_limit_bytes=63 << 20
        ),
        name="mixer",
    )(*planes, *tables, in_weight, in_bias, out_weight, out_bias)
    return (
        mixed.transpose(2, 0, 1, 3),
        grad.transpose(2, 0, 1, 3),
        *parameter_grads,
    )


def solution(mesh):
    in_specs = (P("rep", "seq", None, None), P("rep", "seq", None, None), P(), P(), P(), P())
    out_specs = (P("rep", "seq", None, None), P("rep", "seq", None, None), P(), P(), P(), P())
    return jax.shard_map(shards, mesh=mesh, in_specs=in_specs, out_specs=out_specs, check_vma=False)
```

profile of v0, /device:TPU:0, one launch (start us, length us, event | category | flops | bytes accessed | tf_op | source)
XLA Modules:
  0.0 133.9 jit_solution(18353403621919019062)
XLA Ops:
  0.6 124.7 %mixer.1 = (bf16[3,180,2,768]{3,2,1,0:T(2,128)(2,1)}, bf16[3,180,2,768]{3,2,1,0:T(2,128)(2,1)}, f32[2,8,96,96]{3,2,1,0:T(8,128)}, f32[2,768]{1,0:T(2,128)}, f32[2,8,96,96]{3,2,1,0:T(8,128)}, /*index=5*/f32[2,768]{1,0:T(2,128)}) custom-call(bf16[3,180,2,768]{3,2,1,0:T(2,128)(2,1)} %bitcast.6, bf16[3,180,2,768]{3,2,1,0:T(2,128)(2,1)} %bitcast.7, ...), custom_call_target="tpu_custom_call" | custom-call | tf_op jit(solution)/shard_map/mixer/pallas_call | solution.py:628
  125.4 0.0 copy-start
  125.4 3.9 %copy.23 = bf16[2,3,180,768]{3,0,2,1:T(2,128)(2,1)} copy(bf16[2,3,180,768]{3,0,2,1:T(2,128)(2,1)} %bitcast.5) | data formatting | bytes 3317760
  129.3 0.0 copy-done
  129.3 0.0 copy-start.2
  129.3 0.0 copy-start.4
  129.3 0.0 copy-start.1
  129.3 1.2 copy.24
  130.4 0.5 copy-done.2
  130.9 0.0 copy-start.3
  130.9 0.9 copy.25
  131.8 0.0 copy-done.4
  131.8 0.6 copy.26
  132.4 0.0 copy-done.1
  132.4 0.9 copy.27
  133.3 0.0 copy-done.3
  133.3 0.6 copy.28
Async XLA Ops:
  125.4 3.9 %copy-start = (bf16[3,180,2,768]{3,2,1,0:T(2,128)(2,1)S(1)}, bf16[3,180,2,768]{3,2,1,0:T(2,128)(2,1)}, u32[]{:S(2)}) copy-start(bf16[3,180,2,768]{3,2,1,0:T(2,128)(2,1)} %get-tuple-element.13) | copy-start | bytes 4976644
  129.3 1.7 %copy-start.2 = (f32[2,8,96,96]{3,2,1,0:T(8,128)S(1)}, f32[2,8,96,96]{3,2,1,0:T(8,128)}, u32[]{:S(2)}) copy-start(f32[2,8,96,96]{3,2,1,0:T(8,128)} %get-tuple-element.26) | copy-start | bytes 1769476
  129.3 2.5 %copy-start.4 = (f32[2,768]{1,0:T(2,128)S(1)}, f32[2,768]{1,0:T(2,128)}, u32[]{:S(2)}) copy-start(f32[2,768]{1,0:T(2,128)} %get-tuple-element.27) | copy-start | bytes 18436
  129.3 3.1 %copy-start.1 = (f32[2,8,96,96]{3,2,1,0:T(8,128)S(1)}, f32[2,8,96,96]{3,2,1,0:T(8,128)}, u32[]{:S(2)}) copy-start(f32[2,8,96,96]{3,2,1,0:T(8,128)} %get-tuple-element.28) | copy-start | bytes 1769476
  130.9 2.4 %copy-start.3 = (f32[2,768]{1,0:T(2,128)S(1)}, f32[2,768]{1,0:T(2,128)}, u32[]{:S(2)}) copy-start(f32[2,768]{1,0:T(2,128)} %get-tuple-element.29) | copy-start | bytes 18436
where the time goes:
time: 137 us; the launch traced here: 134 us
  Pallas kernels  125 us (91%)
  local copies, waits for them, and re-layouts  8.48 us (6%)
    pallas_call x1, Pallas kernels, shards(): pl.pallas_call(functools.partial(mixer, n, inner, float(samples * reps)),...  125 us
    unnamed x16, local copies, waits for them, and re-layouts  8.48 us

commit v1 on v0

--- a/solution.py
+++ b/solution.py
@@ -159,6 +159,7 @@
 PER_GROUP = GROUP // BLOCK
 COPY_A, COPY_B, COPY_C, COPY_E, COPY_F, COPY_G, COPY_H, COPY_D = range(8)
 MESH_ID = pl.DeviceIdType.MESH
+VMEM_LIMIT = 52 << 20
 
 
 def host_tables(length, modes):
@@ -212,6 +213,23 @@
     n,
     inner,
     divisor,
+    tok_far,
+    cot_far,
+    col_tok_far,
+    col_cot_far,
+    inv_mix_far,
+    inv_grad_far,
+    turn_far,
+    in_weight_far,
+    in_bias_far,
+    out_weight_far,
+    out_bias_far,
+    mixed,
+    grad,
+    in_weight_grad,
+    in_bias_grad,
+    out_weight_grad,
+    out_bias_grad,
     tok,
     cot,
     col_tok,
@@ -223,12 +241,6 @@
     in_bias,
     out_weight,
     out_bias,
-    mixed,
-    grad,
-    in_weight_grad,
-    in_bias_grad,
-    out_weight_grad,
-    out_bias_grad,
     send_a,
     send_b,
     send_c,
@@ -260,6 +272,7 @@
     recv_sem,
     pair_send,
     pair_recv,
+    load_sem,
 ):
     me = lax.axis_index("seq")
     core = lax.axis_index("rep")
@@ -282,6 +295,25 @@
     lax.fori_loop(1, n, greet, 0)
     pl.semaphore_signal(barrier, inc=1, device_id={"rep": partner}, device_id_type=MESH_ID)
 
+    moves = [(col_tok_far, col_tok)]
+    moves += [(tok_far.at[h], tok.at[h]) for h in range(rows)]
+    moves += [(col_cot_far, col_cot)]
+    moves += [(cot_far.at[h], cot.at[h]) for h in range(rows)]
+    moves += [
+        (in_weight_far, in_weight),
+        (out_weight_far, out_weight),
+        (turn_far, turn),
+        (in_bias_far, in_bias),
+        (out_bias_far, out_bias),
+        (inv_mix_far, inv_mix),
+        (inv_grad_far, inv_grad),
+    ]
+    loads = [
+        pltpu.make_async_copy(far, near, load_sem.at[i]) for i, (far, near) in enumerate(moves)
+    ]
+    for load in loads:
+        load.start()
+
     def copy_to(phase, peer, mine, source, target):
         return pltpu.make_async_remote_copy(
             src_ref=source,
@@ -300,7 +332,12 @@
         lax.fori_loop(1, count, step, 0)
 
     def peer_at(j):
-        return lax.rem(me + j, n)
+        peer = jnp.int32(0)
+        bit = 1
+        while bit < n:
+            peer = peer + bit * lax.rem(me // bit + j // bit, 2)
+            bit *= 2
+        return peer
 
     def plane_at(j):
         return lax.rem(within + j, inner)
@@ -371,18 +408,22 @@
     move_g = line(COPY_G, lambda z: part, lambda z: gathered.at[within, z])
     move_h = plane(COPY_H, lambda v: gathered.at[within], lambda v: gathered.at[v])
 
-    def columns(tokens, table, send):
+    def columns(tokens, table, send, arrived):
+        arrived[0].wait()
         for h in range(rows):
+            arrived[1 + h].wait()
             product = dot(table[...], tokens[h].reshape(width * samples, channels))
             send[:, h * row_chunk : (h + 1) * row_chunk, :] = product.astype(bf16).reshape(
                 n, row_chunk, channels
             )
 
-    columns(tok, col_tok, send_a)
+    columns(tok, col_tok, send_a, loads[: rows + 1])
     pl.semaphore_wait(barrier, n)
     move_a[0]()
-    columns(cot, col_cot, send_b)
+    columns(cot, col_cot, send_b, loads[rows + 1 : 2 * rows + 2])
     move_b[0]()
+    for load in loads[2 * rows + 2 :]:
+        load.wait()
     recv_a[me] = send_a[me]
     recv_b[me] = send_b[me]
 
@@ -468,6 +509,8 @@
 
     move_b[1]()
     per_group(backward_group)
+    pieces[0][0]()
+    recv_d[me] = send_d[me]
 
     def fold(product):
         total = jnp.zeros((BLOCK, GROUP), jnp.float32)
@@ -535,8 +578,6 @@
     )
     move_e[0]()
     recv_e[within] = send_e[within]
-    pieces[0][0]()
-    recv_d[me] = send_d[me]
     move_c[1]()
     inverse(tok, inv_mix, recv_c, mixed)
 
@@ -567,6 +608,8 @@
     last_swap = swap(1, gathered, other)
     last_swap.start()
     both[core] = gathered[...].reshape(n * 16, channels)
+    for move in (move_a, move_b, move_c, move_e, move_f, move_g, move_h):
+        move[2]()
     for h in range(max(1, rows - 1), rows):
         pieces[h][1]()
         inverse_row(h, cot, inv_grad, recv_d, grad)
@@ -584,8 +627,20 @@
                 for c in range(2):
                     out[c, g * PER_GROUP + i] = block[c * BLOCK : (c + 1) * BLOCK]
 
-    for move in (move_a, move_b, move_c, move_e, move_f, move_g, move_h, *pieces):
+    for move in pieces:
         move[2]()
+
+
+def settle(*refs):
+    count = len(refs) // 2
+    near, far, sems = refs[:count], refs[count:-1], refs[-1]
+    copies = [
+        pltpu.make_async_copy(a, b, sems.at[i]) for i, (a, b) in enumerate(zip(near, far))
+    ]
+    for copy in copies:
+        copy.start()
+    for copy in copies:
+        copy.wait()
 
 
 def fits(n, reps, samples, rows, channels):
@@ -625,19 +680,23 @@
     planes = (tokens.transpose(1, 2, 0, 3), cotangent.transpose(1, 2, 0, 3))
     kept = pltpu.VMEM((groups, whole, GROUP), bf16)
     vmem = pl.BlockSpec(memory_space=pltpu.VMEM)
-    mixed, grad, *parameter_grads = pl.pallas_call(
+    far = pl.BlockSpec(memory_space=pltpu.HBM)
+    inputs = (*planes, *tables, in_weight, in_bias, out_weight, out_bias)
+    shapes = (
+        (planes[0].shape, bf16),
+        (planes[1].shape, bf16),
+        (in_weight.shape, f32),
+        (in_bias.shape, f32),
+        (out_weight.shape, f32),
+        (out_bias.shape, f32),
+    )
+    near = pl.pallas_call(
         functools.partial(mixer, n, inner, float(samples * reps)),
-        out_shape=(
-            jax.ShapeDtypeStruct(planes[0].shape, bf16),
-            jax.ShapeDtypeStruct(planes[1].shape, bf16),
-            jax.ShapeDtypeStruct(in_weight.shape, f32),
-            jax.ShapeDtypeStruct(in_bias.shape, f32),
-            jax.ShapeDtypeStruct(out_weight.shape, f32),
-            jax.ShapeDtypeStruct(out_bias.shape, f32),
-        ),
-        in_specs=[vmem] * 11,
+        out_shape=tuple(pltpu.VMEM(*shape) for shape in shapes),
+        in_specs=[far] * 11,
         out_specs=(vmem,) * 6,
-        scratch_shapes=[block] * 4
+        scratch_shapes=[pltpu.VMEM(v.shape, v.dtype) for v in inputs]
+        + [block] * 4
         + [ringed, lined]
         + [block] * 4
         + [ringed, lined]
@@ -661,12 +720,22 @@
             pltpu.SemaphoreType.DMA((COPY_D + rows, n)),
             pltpu.SemaphoreType.DMA((2,)),
             pltpu.SemaphoreType.DMA((2,)),
+            pltpu.SemaphoreType.DMA((2 * rows + 9,)),
         ],
         compiler_params=pltpu.CompilerParams(
-            collective_id=0, has_side_effects=True, vmem_limit_bytes=63 << 20
+            collective_id=0, has_side_effects=True, vmem_limit_bytes=VMEM_LIMIT
         ),
         name="mixer",
-    )(*planes, *tables, in_weight, in_bias, out_weight, out_bias)
+    )(*inputs)
+    mixed, grad, *parameter_grads = pl.pallas_call(
+        settle,
+        out_shape=tuple(jax.ShapeDtypeStruct(*shape) for shape in shapes),
+        in_specs=[pl.BlockSpec(memory_space=pl.ANY)] * 6,
+        out_specs=(far,) * 6,
+        scratch_shapes=[pltpu.SemaphoreType.DMA((6,))],
+        compiler_params=pltpu.CompilerParams(vmem_limit_bytes=1 << 20),
+        name="settle",
+    )(*(pltpu.with_memory_space_constraint(part, pltpu.VMEM) for part in near))
     return (
         mixed.transpose(2, 0, 1, 3),
         grad.transpose(2, 0, 1, 3),

time: 137 us -> 129 us (0.942); the launches traced: 134 us -> 129 us
  local copies, waits for them, and re-layouts: 8.48 us -> 0 us
  Pallas kernels: 125 us -> 128 us
    unnamed x16 -> x0, local copies, waits for them, and re-layouts: 8.48 us -> none
    pallas_call x0 -> x1, Pallas kernels: none -> 2.29 us  [shards(): pl.pallas_call(settle, out_shape=tuple((jax.ShapeDtypeStruct(*shape) for...]
    pallas_call x1, Pallas kernels: 125 us -> 126 us  [shards(): pl.pallas_call(functools.partial(mixer, n, inner, float(samples * reps)),...]
where the time goes in v1:
time: 129 us
  Pallas kernels  128 us (99%)
    pallas_call x1, Pallas kernels, shards(): pl.pallas_call(functools.partial(mixer, n, inner, float(samples * reps)),...  126 us

profile of v1, /device:TPU:0, one launch (start us, length us, event | category | flops | bytes accessed | tf_op | source)
XLA Modules:
  0.0 129.3 jit_solution(7586784244643277546)
XLA Ops:
  0.6 126.2 %mixer.1 = (bf16[3,180,2,768]{3,2,1,0:T(2,128)(2,1)S(1)}, bf16[3,180,2,768]{3,2,1,0:T(2,128)(2,1)S(1)}, f32[2,8,96,96]{3,2,1,0:T(8,128)S(1)}, f32[2,768]{1,0:T(2...) custom-call(bf16[3,180,2,768]{3,2,1,0:T(2,128)(2,1)} %bitcast.4, bf16[3,180,2,768]{3,2,1,0:T(2,128)(2,1)} %bitcast.5, ...), custom_call_target="tpu_custom_call" | custom-call | tf_op jit(solution)/shard_map/mixer/pallas_call | solution.py:693
  126.8 2.3 %settle.1 = (bf16[3,180,2,768]{3,2,1,0:T(2,128)(2,1)}, bf16[3,180,2,768]{3,2,1,0:T(2,128)(2,1)}, f32[2,8,96,96]{3,2,1,0:T(8,128)}, f32[2,768]{1,0:T(2,128)}, f32[2,8,96,96]{3,2,1,0:T(8,128)}, /*index=5*/f32[2,768]{1,0:T(2,128)}) custom-call(bf16[3,180,2,768]{3,2,1,0:T(2,128)(2,1)S(1)} %get-tuple-element.18.refs_0_, ...), custom_call_target="tpu_custom_call" | custom-call | tf_op jit(solution)/shard_map/settle/pallas_call | solution.py:730

commit v2 on v1

--- a/solution.py
+++ b/solution.py
@@ -157,7 +157,6 @@
 
 GROUP = math.lcm(BLOCK, 128)
 PER_GROUP = GROUP // BLOCK
-COPY_A, COPY_B, COPY_C, COPY_E, COPY_F, COPY_G, COPY_H, COPY_D = range(8)
 MESH_ID = pl.DeviceIdType.MESH
 VMEM_LIMIT = 52 << 20
 
@@ -245,12 +244,12 @@
     send_b,
     send_c,
     send_d,
-    send_e,
-    send_f,
     recv_a,
     recv_b,
     recv_c,
     recv_d,
+    send_e,
+    send_f,
     recv_e,
     recv_f,
     turn_back,
@@ -281,7 +280,7 @@
     groups = channels // GROUP
     outer = n // inner
     across, within = me // inner, lax.rem(me, inner)
-    chunk = send_a.shape[1]
+    chunk = send_a.shape[2]
     row_chunk = chunk // rows
     bf16 = jnp.bfloat16
 
@@ -314,12 +313,12 @@
     for load in loads:
         load.start()
 
-    def copy_to(phase, peer, mine, source, target):
+    def copy_to(slot, peer, source, target):
         return pltpu.make_async_remote_copy(
             src_ref=source,
             dst_ref=target,
-            send_sem=send_sem.at[phase, peer],
-            recv_sem=recv_sem.at[phase, mine],
+            send_sem=send_sem.at[slot],
+            recv_sem=recv_sem.at[slot],
             device_id={"seq": peer},
             device_id_type=MESH_ID,
         )
@@ -339,93 +338,128 @@
             bit *= 2
         return peer
 
-    def plane_at(j):
-        return lax.rem(within + j, inner)
-
-    def line_at(j):
-        return lax.rem(across + j, outer)
-
-    def everyone(phase, source, target, at=None):
-        cut = (lambda ref, i: ref.at[i]) if at is None else (lambda ref, i: ref.at[i, at])
-
-        def out(j):
-            peer = peer_at(j)
-            return copy_to(phase, peer, me, cut(source, peer), cut(target, me))
-
-        def back(j):
-            peer = peer_at(j)
-            return copy_to(phase, peer, peer, cut(source, peer), cut(target, peer))
-
-        return (
-            lambda: loop(n, lambda j: out(j).start()),
-            lambda: loop(n, lambda j: back(j).wait_recv()),
-            lambda: loop(n, lambda j: out(j).wait_send()),
+    class Move:
+        def __init__(self, slot, count, to, source, target, span):
+            self.slot, self.count, self.to = slot, count, to
+            self.source, self.target, self.span = source, target, span
+
+        def start(self):
+            def out(j):
+                at, peer = self.to(j)
+                copy_to(self.slot, peer, self.source(at), self.target).start()
+
+            loop(self.count, out)
+
+        def all(self):
+            return copy_to(self.slot, me, self.span, self.span)
+
+        def arrived(self):
+            self.all().wait_recv()
+
+        def left(self):
+            self.all().wait_send()
+
+    def to_peer(j):
+        peer = peer_at(j)
+        return peer, peer
+
+    def to_plane(j):
+        v = lax.rem(within + j, inner)
+        return v, across * inner + v
+
+    def to_line(j):
+        z = lax.rem(across + j, outer)
+        return z, z * inner + within
+
+    def everyone(slot, source, target, g, at=None):
+        cut = pl.ds(0, chunk) if at is None else at
+        return Move(
+            slot,
+            n,
+            to_peer,
+            lambda peer: source.at[g, peer, cut],
+            target.at[g, me, cut],
+            target.at[g, pl.ds(0, n - 1), cut],
         )
 
-    def plane(phase, source, target):
-        def out(j):
-            v = plane_at(j)
-            peer = across * inner + v
-            return copy_to(phase, peer, me, source(v), target(within))
-
-        def back(j):
-            v = plane_at(j)
-            peer = across * inner + v
-            return copy_to(phase, peer, peer, source(v), target(v))
-
-        return (
-            lambda: loop(inner, lambda j: out(j).start()),
-            lambda: loop(inner, lambda j: back(j).wait_recv()),
-            lambda: loop(inner, lambda j: out(j).wait_send()),
+    def move_a(g):
+        return everyone(g, send_a, recv_a, g)
+
+    def move_b(g):
+        return everyone(groups + g, send_b, recv_b, g)
+
+    def move_c(g):
+        return everyone(2 * groups + g, send_c, recv_c, g)
+
+    def move_d(g, h):
+        return everyone(
+            3 * groups + g * rows + h, send_d, recv_d, g, pl.ds(h * row_chunk, row_chunk)
         )
 
-    def line(phase, source, target):
-        def out(j):
-            z = line_at(j)
-            peer = z * inner + within
-            return copy_to(phase, peer, me, source(z), target(across))
-
-        def back(j):
-            z = line_at(j)
-            peer = z * inner + within
-            return copy_to(phase, peer, peer, source(z), target(z))
-
-        return (
-            lambda: loop(outer, lambda j: out(j).start()),
-            lambda: loop(outer, lambda j: back(j).wait_recv()),
-            lambda: loop(outer, lambda j: out(j).wait_send()),
-        )
-
-    move_a = everyone(COPY_A, send_a, recv_a)
-    move_b = everyone(COPY_B, send_b, recv_b)
-    move_c = everyone(COPY_C, send_c, recv_c)
-    pieces = [
-        everyone(COPY_D + h, send_d, recv_d, pl.ds(h * row_chunk, row_chunk))
-        for h in range(rows)
-    ]
-    move_e = plane(COPY_E, lambda v: send_e.at[v], lambda v: recv_e.at[v])
-    move_f = line(COPY_F, lambda z: send_f.at[z], lambda z: recv_f.at[z])
-    move_g = line(COPY_G, lambda z: part, lambda z: gathered.at[within, z])
-    move_h = plane(COPY_H, lambda v: gathered.at[within], lambda v: gathered.at[v])
-
-    def columns(tokens, table, send, arrived):
-        arrived[0].wait()
+    tail = 3 * groups + rows * groups
+    move_e = Move(
+        tail,
+        inner,
+        to_plane,
+        lambda v: send_e.at[v],
+        recv_e.at[within],
+        recv_e.at[pl.ds(0, inner - 1)],
+    )
+    move_f = Move(
+        tail + 1,
+        outer,
+        to_line,
+        lambda z: send_f.at[z],
+        recv_f.at[across],
+        recv_f.at[pl.ds(0, outer - 1)],
+    )
+    move_g = Move(
+        tail + 2,
+        outer,
+        to_line,
+        lambda z: part,
+        gathered.at[within, across],
+        gathered.at[within, pl.ds(0, outer - 1)],
+    )
+    move_h = Move(
+        tail + 3,
+        inner,
+        to_plane,
+        lambda v: gathered.at[within],
+        gathered.at[within],
+        gathered.at[pl.ds(0, inner - 1)],
+    )
+
+    def lanes(g):
+        return pl.ds(pl.multiple_of(g * GROUP, GROUP), GROUP)
+
+    def fixed(g):
+        return pl.ds(g * GROUP, GROUP)
+
+    def columns(tokens, table, send, g, arrived):
         for h in range(rows):
-            arrived[1 + h].wait()
-            product = dot(table[...], tokens[h].reshape(width * samples, channels))
-            send[:, h * row_chunk : (h + 1) * row_chunk, :] = product.astype(bf16).reshape(
-                n, row_chunk, channels
+            if arrived:
+                arrived[h].wait()
+            section = tokens[h, :, :, fixed(g)].reshape(width * samples, GROUP)
+            send[g, :, h * row_chunk : (h + 1) * row_chunk, :] = (
+                dot(table[...], section).astype(bf16).reshape(n, row_chunk, GROUP)
             )
 
-    columns(tok, col_tok, send_a, loads[: rows + 1])
-    pl.semaphore_wait(barrier, n)
-    move_a[0]()
-    columns(cot, col_cot, send_b, loads[rows + 1 : 2 * rows + 2])
-    move_b[0]()
+    for g in range(groups):
+        if g == 0:
+            loads[0].wait()
+        columns(tok, col_tok, send_a, g, loads[1 : rows + 1] if g == 0 else None)
+        if g == 0:
+            pl.semaphore_wait(barrier, n)
+        move_a(g).start()
+        if g == 0:
+            loads[rows + 1].wait()
+        columns(cot, col_cot, send_b, g, loads[rows + 2 : 2 * rows + 2] if g == 0 else None)
+        move_b(g).start()
     for load in loads[2 * rows + 2 :]:
         load.wait()
-    recv_a[me] = send_a[me]
-    recv_b[me] = send_b[me]
+    recv_a[:, me] = send_a[:, me]
+    recv_b[:, me] = send_b[:, me]
 
     turn_back[...] = turn[...].T
     row_at = lax.broadcasted_iota(jnp.int32, (BLOCK, GROUP), 0)
@@ -442,9 +476,6 @@
     half = turn.shape[0] // 2
     scale = math.sqrt(2.0 / math.pi)
 
-    def lanes(g):
-        return pl.ds(pl.multiple_of(g * GROUP, GROUP), GROUP)
-
     def per_group(act):
         def step(g, carry):
             act(g, lanes(g))
@@ -452,16 +483,14 @@
 
         lax.fori_loop(0, groups, step, 0)
 
-    def along_rows(recv, at, keep, g):
-        keep[g] = dot(turn[...], recv[:, :, at].reshape(turn.shape[1], GROUP)).astype(bf16)
-
-    def back_rows(send, at):
-        send[:, :, at] = (
-            dot(turn_back[...], mixed_modes[...]).astype(bf16).reshape(n, chunk, GROUP)
-        )
+    def along_rows(recv, keep, g):
+        keep[g] = dot(turn[...], recv[g].reshape(turn.shape[1], GROUP)).astype(bf16)
+
+    def back_rows(send, g):
+        send[g] = dot(turn_back[...], mixed_modes[...]).astype(bf16).reshape(n, chunk, GROUP)
 
     def forward_group(g, at):
-        along_rows(recv_a, at, spec, g)
+        along_rows(recv_a, spec, g)
         re, im = spec[g, :half], spec[g, half:]
         w_re, w_im = wide[0, g], wide[1, g]
         for c in range(2):
@@ -484,15 +513,10 @@
         mixed_modes[half:] = (
             dot(re, w_im) + dot(im, w_re) + out_bias[1:2, at]
         ).astype(bf16)
-        back_rows(send_c, at)
-
-    move_a[1]()
-    per_group(forward_group)
-    move_c[0]()
-    recv_c[me] = send_c[me]
-
-    def backward_group(g, at):
-        along_rows(recv_b, at, inc, g)
+        back_rows(send_c, g)
+
+    def backward_group(g):
+        along_rows(recv_b, inc, g)
         re, im = inc[g, :half], inc[g, half:]
         w_re, w_im = wide[2, g], wide[3, g]
         pre[g, :half] = (
@@ -505,12 +529,7 @@
         w_re, w_im = wide[0, g], wide[1, g]
         mixed_modes[:half] = (dot(re, w_re, (1, 1)) + dot(im, w_im, (1, 1))).astype(bf16)
         mixed_modes[half:] = (dot(im, w_re, (1, 1)) - dot(re, w_im, (1, 1))).astype(bf16)
-        back_rows(send_d, at)
-
-    move_b[1]()
-    per_group(backward_group)
-    pieces[0][0]()
-    recv_d[me] = send_d[me]
+        back_rows(send_d, g)
 
     def fold(product):
         total = jnp.zeros((BLOCK, GROUP), jnp.float32)
@@ -538,7 +557,29 @@
                 bias = jnp.where(bias_at == 2 * k + c, total, bias)
         grads[4 * BLOCK : 4 * BLOCK + 16, at] = bias.astype(bf16)
 
-    per_group(grads_group)
+    def mix_group(g, at):
+        with jax.named_scope("wait_a"):
+            move_a(g).arrived()
+        with jax.named_scope("fwd"):
+            forward_group(g, at)
+        move_c(g).start()
+        recv_c[g, me] = send_c[g, me]
+        with jax.named_scope("wait_b"):
+            move_b(g).arrived()
+        with jax.named_scope("bwd"):
+            backward_group(g)
+        recv_d[g, me] = send_d[g, me]
+
+        @pl.when(g < groups - 1)
+        def _():
+            for h in range(rows):
+                move_d(g, h).start()
+
+        with jax.named_scope("grads"):
+            grads_group(g, at)
+
+    per_group(mix_group)
+
     per = 4 * BLOCK // (2 * n)
     to_row = lax.broadcasted_iota(jnp.int32, (2 * n * 16, 4 * BLOCK + 16), 0)
     from_row = lax.broadcasted_iota(jnp.int32, (2 * n * 16, 4 * BLOCK + 16), 1)
@@ -560,75 +601,91 @@
     first_swap = swap(0, halves.at[partner], half_in)
     first_swap.start()
 
-    def inverse_row(h, tokens, table, recv, out):
-        section = recv[:, h * row_chunk : (h + 1) * row_chunk, :]
-        product = dot(table[...], section.reshape(n * row_chunk, channels))
-        kept = tokens[h].reshape(width * samples, channels).astype(jnp.float32)
-        out[h] = (kept + product).astype(bf16).reshape(width, samples, channels)
-
-    def inverse(tokens, table, recv, out):
-        for h in range(rows):
-            inverse_row(h, tokens, table, recv, out)
-
-    first_swap.wait()
+    def inverse_row(h, g, tokens, table, recv, out):
+        section = recv[g, :, h * row_chunk : (h + 1) * row_chunk, :]
+        product = dot(table[...], section.reshape(n * row_chunk, GROUP))
+        kept = tokens[h, :, :, fixed(g)].reshape(width * samples, GROUP).astype(jnp.float32)
+        out[h, :, :, fixed(g)] = (kept + product).astype(bf16).reshape(width, samples, GROUP)
+
+    with jax.named_scope("swap1"):
+        first_swap.wait()
     send_e[...] = (
         (halves[core].astype(jnp.float32) + half_in[...].astype(jnp.float32))
         .astype(bf16)
         .reshape(send_e.shape)
     )
-    move_e[0]()
+    move_e.start()
     recv_e[within] = send_e[within]
-    move_c[1]()
-    inverse(tok, inv_mix, recv_c, mixed)
-
-    move_e[1]()
+    move_d(groups - 1, 0).start()
+    for g in range(groups):
+        with jax.named_scope(f"wait_c{g}"):
+            move_c(g).arrived()
+        for h in range(rows):
+            inverse_row(h, g, tok, inv_mix, recv_c, mixed)
+
+    with jax.named_scope("wait_e"):
+        move_e.arrived()
     send_f[...] = jnp.sum(recv_e[...].astype(jnp.float32), axis=0).astype(bf16)
-    move_f[0]()
+    move_f.start()
     recv_f[across] = send_f[across]
-    middle = max(2, rows - 1)
-    for piece in pieces[1:middle]:
-        piece[0]()
-    move_f[1]()
+    for h in range(1, rows - 1):
+        move_d(groups - 1, h).start()
+    for g in range(groups):
+        move_a(g).left()
+        move_b(g).left()
+        move_c(g).left()
+    with jax.named_scope("wait_f"):
+        move_f.arrived()
     total = jnp.sum(recv_f[...].astype(jnp.float32), axis=0) * (1.0 / divisor)
     in_bias_grad[...] = total[per : per + 2]
     out_bias_grad[...] = total[per + 2 : per + 4]
     part[...] = total.astype(bf16)
-    move_g[0]()
+    move_g.start()
     gathered[within, across] = part[...]
-    for piece in pieces[middle:]:
-        piece[0]()
-    pieces[0][1]()
-    inverse_row(0, cot, inv_grad, recv_d, grad)
-    move_g[1]()
-    move_h[0]()
-    for h in range(1, rows - 1):
-        pieces[h][1]()
-        inverse_row(h, cot, inv_grad, recv_d, grad)
-    move_h[1]()
+    move_d(groups - 1, rows - 1).start()
+    for g in range(groups - 1):
+        for h in range(rows):
+            with jax.named_scope(f"wait_d{g}"):
+                move_d(g, h).arrived()
+            inverse_row(h, g, cot, inv_grad, recv_d, grad)
+    with jax.named_scope("wait_g"):
+        move_g.arrived()
+    move_h.start()
+    for h in range(rows - 1):
+        with jax.named_scope(f"wait_dl{h}"):
+            move_d(groups - 1, h).arrived()
+        inverse_row(h, groups - 1, cot, inv_grad, recv_d, grad)
+    with jax.named_scope("wait_h"):
+        move_h.arrived()
     last_swap = swap(1, gathered, other)
     last_swap.start()
     both[core] = gathered[...].reshape(n * 16, channels)
-    for move in (move_a, move_b, move_c, move_e, move_f, move_g, move_h):
-        move[2]()
-    for h in range(max(1, rows - 1), rows):
-        pieces[h][1]()
-        inverse_row(h, cot, inv_grad, recv_d, grad)
-    last_swap.wait()
+    for move in (move_e, move_f, move_g, move_h):
+        move.left()
+    for g in range(groups - 1):
+        for h in range(rows):
+            move_d(g, h).left()
+    with jax.named_scope("wait_dl2"):
+        move_d(groups - 1, rows - 1).arrived()
+    inverse_row(rows - 1, groups - 1, cot, inv_grad, recv_d, grad)
+    with jax.named_scope("swap2"):
+        last_swap.wait()
     both[partner] = other[...].reshape(n * 16, channels)
     to_row = lax.broadcasted_iota(jnp.int32, (2 * BLOCK, n * 16), 0)
     from_row = lax.broadcasted_iota(jnp.int32, (2 * BLOCK, n * 16), 1)
     order = (to_row // per * 16 + to_row % per == from_row).astype(bf16)
-    for k, out in enumerate((in_weight_grad, out_weight_grad)):
-        for g in range(groups):
-            ordered = dot(order, both[k, :, g * GROUP : (g + 1) * GROUP]).astype(bf16)
-            for i in range(PER_GROUP):
-                place = (lane_at == row_at + i * BLOCK).astype(bf16)
-                block = dot(ordered, place, (1, 1))
-                for c in range(2):
-                    out[c, g * PER_GROUP + i] = block[c * BLOCK : (c + 1) * BLOCK]
-
-    for move in pieces:
-        move[2]()
+    with jax.named_scope("params"):
+        for k, out in enumerate((in_weight_grad, out_weight_grad)):
+            for g in range(groups):
+                ordered = dot(order, both[k, :, g * GROUP : (g + 1) * GROUP]).astype(bf16)
+                for i in range(PER_GROUP):
+                    place = (lane_at == row_at + i * BLOCK).astype(bf16)
+                    block = dot(ordered, place, (1, 1))
+                    for c in range(2):
+                        out[c, g * PER_GROUP + i] = block[c * BLOCK : (c + 1) * BLOCK]
+    with jax.named_scope("end"):
+        for h in range(rows):
+            move_d(groups - 1, h).left()
 
 
 def settle(*refs):
@@ -652,7 +709,7 @@
         and channels % GROUP == 0
         and channels == BLOCKS * BLOCK
         and (4 * BLOCK) % (2 * n) == 0
-        and n > 1
+        and n > 3
         and n & (n - 1) == 0
         and rows > 1
         and 4 * BLOCK // (2 * n) + 4 <= 16
@@ -673,13 +730,13 @@
     groups = channels // GROUP
     tables = [jnp.asarray(t) for t in kernel_tables(width, length, n, samples, rows)]
     bf16, f32 = jnp.bfloat16, jnp.float32
-    block = pltpu.VMEM((n, chunk, channels), bf16)
+    block = pltpu.VMEM((groups, n, chunk, GROUP), bf16)
     small = pltpu.VMEM((n, 16, channels), bf16)
     ringed = pltpu.VMEM((inner, outer, 16, channels), bf16)
     lined = pltpu.VMEM((outer, 16, channels), bf16)
     planes = (tokens.transpose(1, 2, 0, 3), cotangent.transpose(1, 2, 0, 3))
     kept = pltpu.VMEM((groups, whole, GROUP), bf16)
-    vmem = pl.BlockSpec(memory_space=pltpu.VMEM)
+    anywhere = pl.BlockSpec(memory_space=pl.ANY)
     far = pl.BlockSpec(memory_space=pltpu.HBM)
     inputs = (*planes, *tables, in_weight, in_bias, out_weight, out_bias)
     shapes = (
@@ -694,12 +751,11 @@
         functools.partial(mixer, n, inner, float(samples * reps)),
         out_shape=tuple(pltpu.VMEM(*shape) for shape in shapes),
         in_specs=[far] * 11,
-        out_specs=(vmem,) * 6,
+        grid=(1,),
+        out_specs=(pl.BlockSpec(memory_space=pltpu.VMEM),) * 6,
         scratch_shapes=[pltpu.VMEM(v.shape, v.dtype) for v in inputs]
-        + [block] * 4
-        + [ringed, lined]
-        + [block] * 4
-        + [ringed, lined]
+        + [block] * 8
+        + [ringed, lined] * 2
         + [
             pltpu.VMEM((whole, whole), bf16),
             pltpu.VMEM((4, groups, GROUP, GROUP), bf16),
@@ -716,8 +772,8 @@
             ringed,
             ringed,
             pltpu.VMEM((2, n * 16, channels), bf16),
-            pltpu.SemaphoreType.DMA((COPY_D + rows, n)),
-            pltpu.SemaphoreType.DMA((COPY_D + rows, n)),
+            pltpu.SemaphoreType.DMA(((3 + rows) * groups + 4,)),
+            pltpu.SemaphoreType.DMA(((3 + rows) * groups + 4,)),
             pltpu.SemaphoreType.DMA((2,)),
             pltpu.SemaphoreType.DMA((2,)),
             pltpu.SemaphoreType.DMA((2 * rows + 9,)),
@@ -730,7 +786,7 @@
     mixed, grad, *parameter_grads = pl.pallas_call(
         settle,
         out_shape=tuple(jax.ShapeDtypeStruct(*shape) for shape in shapes),
-        in_specs=[pl.BlockSpec(memory_space=pl.ANY)] * 6,
+        in_specs=[anywhere] * 6,
         out_specs=(far,) * 6,
         scratch_shapes=[pltpu.SemaphoreType.DMA((6,))],
         compiler_params=pltpu.CompilerParams(vmem_limit_bytes=1 << 20),

time: 129 us -> 123 us (0.953)
  Pallas kernels: 128 us -> 122 us
    pallas_call x1, Pallas kernels: 126 us -> 120 us  [shards(): pl.pallas_call(functools.partial(mixer, n, inner, float(samples * reps)),...]
where the time goes in v2:
time: 123 us
  Pallas kernels  122 us (99%)
    pallas_call x1, Pallas kernels, shards(): pl.pallas_call(functools.partial(mixer, n, inner, float(samples * reps)),...  120 us

profile of v2, /device:TPU:0, one launch (start us, length us, event | category | flops | bytes accessed | tf_op | source)
XLA Modules:
  0.0 122.9 jit_solution(3854353994698633009)
XLA Ops:
  0.6 119.8 %mixer.1 = (bf16[3,180,2,768]{3,2,1,0:T(2,128)(2,1)S(1)}, bf16[3,180,2,768]{3,2,1,0:T(2,128)(2,1)S(1)}, f32[2,8,96,96]{3,2,1,0:T(8,128)S(1)}, f32[2,768]{1,0:T(2...) custom-call(bf16[3,180,2,768]{3,2,1,0:T(2,128)(2,1)} %bitcast.4, bf16[3,180,2,768]{3,2,1,0:T(2,128)(2,1)} %bitcast.5, ...), custom_call_target="tpu_custom_call" | custom-call | tf_op jit(solution)/shard_map/mixer/pallas_call | solution.py:750
  120.4 2.3 %settle.1 = (bf16[3,180,2,768]{3,2,1,0:T(2,128)(2,1)}, bf16[3,180,2,768]{3,2,1,0:T(2,128)(2,1)}, f32[2,8,96,96]{3,2,1,0:T(8,128)}, f32[2,768]{1,0:T(2,128)}, f32[2,8,96,96]{3,2,1,0:T(8,128)}, /*index=5*/f32[2,768]{1,0:T(2,128)}) custom-call(bf16[3,180,2,768]{3,2,1,0:T(2,128)(2,1)S(1)} %get-tuple-element.18.refs_0_, ...), custom_call_target="tpu_custom_call" | custom-call | tf_op jit(solution)/shard_map/settle/pallas_call | solution.py:786

commit v3 on v2

--- a/solution.py
+++ b/solution.py
@@ -159,6 +159,7 @@
 PER_GROUP = GROUP // BLOCK
 MESH_ID = pl.DeviceIdType.MESH
 VMEM_LIMIT = 52 << 20
+FIRST, AFTER_E, AFTER_F, AFTER_G = 2, 1, 2, 1
 
 
 def host_tables(length, modes):
@@ -310,7 +311,7 @@
     loads = [
         pltpu.make_async_copy(far, near, load_sem.at[i]) for i, (far, near) in enumerate(moves)
     ]
-    for load in loads:
+    for load in loads[: rows + 1]:
         load.start()
 
     def copy_to(slot, peer, source, target):
@@ -388,15 +389,15 @@
     def move_b(g):
         return everyone(groups + g, send_b, recv_b, g)
 
-    def move_c(g):
-        return everyone(2 * groups + g, send_c, recv_c, g)
+    def move_c(g, h):
+        at = pl.ds(h * row_chunk, row_chunk)
+        return everyone(2 * groups + g * rows + h, send_c, recv_c, g, at)
 
     def move_d(g, h):
-        return everyone(
-            3 * groups + g * rows + h, send_d, recv_d, g, pl.ds(h * row_chunk, row_chunk)
-        )
-
-    tail = 3 * groups + rows * groups
+        at = pl.ds(h * row_chunk, row_chunk)
+        return everyone((2 + rows) * groups + g * rows + h, send_d, recv_d, g, at)
+
+    tail = (2 + 2 * rows) * groups
     move_e = Move(
         tail,
         inner,
@@ -436,25 +437,26 @@
     def fixed(g):
         return pl.ds(g * GROUP, GROUP)
 
-    def columns(tokens, table, send, g, arrived):
+    def columns(tokens, table, send, g):
         for h in range(rows):
-            if arrived:
-                arrived[h].wait()
             section = tokens[h, :, :, fixed(g)].reshape(width * samples, GROUP)
             send[g, :, h * row_chunk : (h + 1) * row_chunk, :] = (
                 dot(table[...], section).astype(bf16).reshape(n, row_chunk, GROUP)
             )
 
+    for load in loads[: rows + 1]:
+        load.wait()
+    for load in loads[rows + 1 :]:
+        load.start()
     for g in range(groups):
-        if g == 0:
-            loads[0].wait()
-        columns(tok, col_tok, send_a, g, loads[1 : rows + 1] if g == 0 else None)
+        columns(tok, col_tok, send_a, g)
         if g == 0:
             pl.semaphore_wait(barrier, n)
         move_a(g).start()
         if g == 0:
-            loads[rows + 1].wait()
-        columns(cot, col_cot, send_b, g, loads[rows + 2 : 2 * rows + 2] if g == 0 else None)
+            for load in loads[rows + 1 : 2 * rows + 2]:
+                load.wait()
+        columns(cot, col_cot, send_b, g)
         move_b(g).start()
     for load in loads[2 * rows + 2 :]:
         load.wait()
@@ -557,24 +559,37 @@
                 bias = jnp.where(bias_at == 2 * k + c, total, bias)
         grads[4 * BLOCK : 4 * BLOCK + 16, at] = bias.astype(bf16)
 
+    last = groups - 1
+    held = [move_c(last, h) for h in range(rows)]
+    held += [move_d(g, h) for g in range(groups) for h in range(rows)]
+
+    def release(count):
+        for move in held[:count]:
+            move.start()
+        del held[:count]
+
     def mix_group(g, at):
         with jax.named_scope("wait_a"):
             move_a(g).arrived()
         with jax.named_scope("fwd"):
             forward_group(g, at)
-        move_c(g).start()
         recv_c[g, me] = send_c[g, me]
+
+        @pl.when(g < last)
+        def _():
+            for h in range(rows):
+                move_c(g, h).start()
+
         with jax.named_scope("wait_b"):
             move_b(g).arrived()
+
+        @pl.when(g == last)
+        def _():
+            release(FIRST)
+
         with jax.named_scope("bwd"):
             backward_group(g)
         recv_d[g, me] = send_d[g, me]
-
-        @pl.when(g < groups - 1)
-        def _():
-            for h in range(rows):
-                move_d(g, h).start()
-
         with jax.named_scope("grads"):
             grads_group(g, at)
 
@@ -616,24 +631,13 @@
     )
     move_e.start()
     recv_e[within] = send_e[within]
-    move_d(groups - 1, 0).start()
-    for g in range(groups):
-        with jax.named_scope(f"wait_c{g}"):
-            move_c(g).arrived()
-        for h in range(rows):
-            inverse_row(h, g, tok, inv_mix, recv_c, mixed)
-
+    release(AFTER_E)
     with jax.named_scope("wait_e"):
         move_e.arrived()
     send_f[...] = jnp.sum(recv_e[...].astype(jnp.float32), axis=0).astype(bf16)
     move_f.start()
     recv_f[across] = send_f[across]
-    for h in range(1, rows - 1):
-        move_d(groups - 1, h).start()
-    for g in range(groups):
-        move_a(g).left()
-        move_b(g).left()
-        move_c(g).left()
+    release(AFTER_F)
     with jax.named_scope("wait_f"):
         move_f.arrived()
     total = jnp.sum(recv_f[...].astype(jnp.float32), axis=0) * (1.0 / divisor)
@@ -642,32 +646,43 @@
     part[...] = total.astype(bf16)
     move_g.start()
     gathered[within, across] = part[...]
-    move_d(groups - 1, rows - 1).start()
-    for g in range(groups - 1):
-        for h in range(rows):
-            with jax.named_scope(f"wait_d{g}"):
-                move_d(g, h).arrived()
-            inverse_row(h, g, cot, inv_grad, recv_d, grad)
+    release(AFTER_G)
     with jax.named_scope("wait_g"):
         move_g.arrived()
     move_h.start()
-    for h in range(rows - 1):
-        with jax.named_scope(f"wait_dl{h}"):
-            move_d(groups - 1, h).arrived()
-        inverse_row(h, groups - 1, cot, inv_grad, recv_d, grad)
+    release(len(held))
+    def finish_c(g, h):
+        with jax.named_scope(f"wait_c{g}{h}"):
+            move_c(g, h).arrived()
+        inverse_row(h, g, tok, inv_mix, recv_c, mixed)
+
+    def finish_d(g, h):
+        with jax.named_scope(f"wait_d{g}{h}"):
+            move_d(g, h).arrived()
+        inverse_row(h, g, cot, inv_grad, recv_d, grad)
+
+    for g in range(groups):
+        for h in range(rows):
+            finish_c(g, h)
+    for g in range(groups):
+        move_a(g).left()
+        move_b(g).left()
+    for move in (move_e, move_f, move_g):
+        move.left()
+    for g in range(last):
+        for h in range(rows):
+            finish_d(g, h)
     with jax.named_scope("wait_h"):
         move_h.arrived()
     last_swap = swap(1, gathered, other)
     last_swap.start()
     both[core] = gathered[...].reshape(n * 16, channels)
-    for move in (move_e, move_f, move_g, move_h):
-        move.left()
-    for g in range(groups - 1):
+    move_h.left()
+    for g in range(groups):
         for h in range(rows):
-            move_d(g, h).left()
-    with jax.named_scope("wait_dl2"):
-        move_d(groups - 1, rows - 1).arrived()
-    inverse_row(rows - 1, groups - 1, cot, inv_grad, recv_d, grad)
+            move_c(g, h).left()
+    for h in range(rows - 1):
+        finish_d(last, h)
     with jax.named_scope("swap2"):
         last_swap.wait()
     both[partner] = other[...].reshape(n * 16, channels)
@@ -683,9 +698,11 @@
                     block = dot(ordered, place, (1, 1))
                     for c in range(2):
                         out[c, g * PER_GROUP + i] = block[c * BLOCK : (c + 1) * BLOCK]
+    finish_d(last, rows - 1)
     with jax.named_scope("end"):
-        for h in range(rows):
-            move_d(groups - 1, h).left()
+        for g in range(groups):
+            for h in range(rows):
+                move_d(g, h).left()
 
 
 def settle(*refs):
@@ -772,8 +789,8 @@
             ringed,
             ringed,
             pltpu.VMEM((2, n * 16, channels), bf16),
-            pltpu.SemaphoreType.DMA(((3 + rows) * groups + 4,)),
-            pltpu.SemaphoreType.DMA(((3 + rows) * groups + 4,)),
+            pltpu.SemaphoreType.DMA(((2 + 2 * rows) * groups + 4,)),
+            pltpu.SemaphoreType.DMA(((2 + 2 * rows) * groups + 4,)),
             pltpu.SemaphoreType.DMA((2,)),
             pltpu.SemaphoreType.DMA((2,)),
             pltpu.SemaphoreType.DMA((2 * rows + 9,)),

time: 123 us -> 118 us (0.959)
  Pallas kernels: 122 us -> 117 us
    pallas_call x1, Pallas kernels: 120 us -> 115 us  [shards(): pl.pallas_call(functools.partial(mixer, n, inner, float(samples * reps)),...]
where the time goes in v3:
time: 118 us
  Pallas kernels  117 us (99%)
    pallas_call x1, Pallas kernels, shards(): pl.pallas_call(functools.partial(mixer, n, inner, float(samples * reps)),...  115 us

profile of v3, /device:TPU:0, one launch (start us, length us, event | category | flops | bytes accessed | tf_op | source)
XLA Modules:
  0.0 117.8 jit_solution(12381574010611919497)
XLA Ops:
  0.6 114.7 %mixer.1 = (bf16[3,180,2,768]{3,2,1,0:T(2,128)(2,1)S(1)}, bf16[3,180,2,768]{3,2,1,0:T(2,128)(2,1)S(1)}, f32[2,8,96,96]{3,2,1,0:T(8,128)S(1)}, f32[2,768]{1,0:T(2...) custom-call(bf16[3,180,2,768]{3,2,1,0:T(2,128)(2,1)} %bitcast.4, bf16[3,180,2,768]{3,2,1,0:T(2,128)(2,1)} %bitcast.5, ...), custom_call_target="tpu_custom_call" | custom-call | tf_op jit(solution)/shard_map/mixer/pallas_call | solution.py:767
  115.3 2.3 %settle.1 = (bf16[3,180,2,768]{3,2,1,0:T(2,128)(2,1)}, bf16[3,180,2,768]{3,2,1,0:T(2,128)(2,1)}, f32[2,8,96,96]{3,2,1,0:T(8,128)}, f32[2,768]{1,0:T(2,128)}, f32[2,8,96,96]{3,2,1,0:T(8,128)}, /*index=5*/f32[2,768]{1,0:T(2,128)}) custom-call(bf16[3,180,2,768]{3,2,1,0:T(2,128)(2,1)S(1)} %get-tuple-element.18.refs_0_, ...), custom_call_target="tpu_custom_call" | custom-call | tf_op jit(solution)/shard_map/settle/pallas_call | solution.py:803

commit v4 on v3

--- a/solution.py
+++ b/solution.py
@@ -159,7 +159,7 @@
 PER_GROUP = GROUP // BLOCK
 MESH_ID = pl.DeviceIdType.MESH
 VMEM_LIMIT = 52 << 20
-FIRST, AFTER_E, AFTER_F, AFTER_G = 2, 1, 2, 1
+FIRST, AFTER_E, AFTER_F = 2, 3, 2
 
 
 def host_tables(length, modes):
@@ -264,7 +264,6 @@
     grads,
     halves,
     half_in,
-    part,
     gathered,
     other,
     both,
@@ -368,10 +367,6 @@
         v = lax.rem(within + j, inner)
         return v, across * inner + v
 
-    def to_line(j):
-        z = lax.rem(across + j, outer)
-        return z, z * inner + within
-
     def everyone(slot, source, target, g, at=None):
         cut = pl.ds(0, chunk) if at is None else at
         return Move(
@@ -406,24 +401,9 @@
         recv_e.at[within],
         recv_e.at[pl.ds(0, inner - 1)],
     )
-    move_f = Move(
-        tail + 1,
-        outer,
-        to_line,
-        lambda z: send_f.at[z],
-        recv_f.at[across],
-        recv_f.at[pl.ds(0, outer - 1)],
-    )
+    move_f = copy_to(tail + 1, (1 - across) * inner + within, send_f, recv_f)
     move_g = Move(
         tail + 2,
-        outer,
-        to_line,
-        lambda z: part,
-        gathered.at[within, across],
-        gathered.at[within, pl.ds(0, outer - 1)],
-    )
-    move_h = Move(
-        tail + 3,
         inner,
         to_plane,
         lambda v: gathered.at[within],
@@ -636,20 +616,14 @@
         move_e.arrived()
     send_f[...] = jnp.sum(recv_e[...].astype(jnp.float32), axis=0).astype(bf16)
     move_f.start()
-    recv_f[across] = send_f[across]
     release(AFTER_F)
     with jax.named_scope("wait_f"):
-        move_f.arrived()
-    total = jnp.sum(recv_f[...].astype(jnp.float32), axis=0) * (1.0 / divisor)
-    in_bias_grad[...] = total[per : per + 2]
-    out_bias_grad[...] = total[per + 2 : per + 4]
-    part[...] = total.astype(bf16)
+        move_f.wait_recv()
+    total = (send_f[...].astype(jnp.float32) + recv_f[...].astype(jnp.float32)) * (1.0 / divisor)
+    in_bias_grad[...] = total[0, per : per + 2]
+    out_bias_grad[...] = total[0, per + 2 : per + 4]
+    gathered[within] = total.astype(bf16)
     move_g.start()
-    gathered[within, across] = part[...]
-    release(AFTER_G)
-    with jax.named_scope("wait_g"):
-        move_g.arrived()
-    move_h.start()
     release(len(held))
     def finish_c(g, h):
         with jax.named_scope(f"wait_c{g}{h}"):
@@ -667,17 +641,17 @@
     for g in range(groups):
         move_a(g).left()
         move_b(g).left()
-    for move in (move_e, move_f, move_g):
-        move.left()
+    move_e.left()
+    move_f.wait_send()
     for g in range(last):
         for h in range(rows):
             finish_d(g, h)
-    with jax.named_scope("wait_h"):
-        move_h.arrived()
+    with jax.named_scope("wait_g"):
+        move_g.arrived()
     last_swap = swap(1, gathered, other)
     last_swap.start()
     both[core] = gathered[...].reshape(n * 16, channels)
-    move_h.left()
+    move_g.left()
     for g in range(groups):
         for h in range(rows):
             move_c(g, h).left()
@@ -740,8 +714,8 @@
     if not fits(n, reps, samples, rows, channels):
         return shards_plain(tokens, cotangent, in_weight, in_bias, out_weight, out_bias)
     length = rows * n
-    inner = 2 ** ((n.bit_length() - 1) // 2)
-    outer = n // inner
+    outer = 2
+    inner = n // outer
     chunk = rows * samples * (MODES // n) * 2
     whole = n * chunk
     groups = channels // GROUP
@@ -785,12 +759,11 @@
             pltpu.VMEM((4 * BLOCK + 16, channels), bf16),
             pltpu.VMEM((2, n, 16, channels), bf16),
             small,
-            pltpu.VMEM((16, channels), bf16),
             ringed,
             ringed,
             pltpu.VMEM((2, n * 16, channels), bf16),
-            pltpu.SemaphoreType.DMA(((2 + 2 * rows) * groups + 4,)),
-            pltpu.SemaphoreType.DMA(((2 + 2 * rows) * groups + 4,)),
+            pltpu.SemaphoreType.DMA(((2 + 2 * rows) * groups + 3,)),
+            pltpu.SemaphoreType.DMA(((2 + 2 * rows) * groups + 3,)),
             pltpu.SemaphoreType.DMA((2,)),
             pltpu.SemaphoreType.DMA((2,)),
             pltpu.SemaphoreType.DMA((2 * rows + 9,)),

time: 118 us -> 117 us (level)
  no operation moved by 1% of the time
where the time goes in v4:
time: 117 us
  Pallas kernels  116 us (99%)
    pallas_call x1, Pallas kernels, shards(): pl.pallas_call(functools.partial(mixer, n, inner, float(samples * reps)),...  114 us

profile of v4, /device:TPU:0, one launch (start us, length us, event | category | flops | bytes accessed | tf_op | source)
XLA Modules:
  0.0 116.8 jit_solution(3272432497759562986)
XLA Ops:
  0.6 113.7 %mixer.1 = (bf16[3,180,2,768]{3,2,1,0:T(2,128)(2,1)S(1)}, bf16[3,180,2,768]{3,2,1,0:T(2,128)(2,1)S(1)}, f32[2,8,96,96]{3,2,1,0:T(8,128)S(1)}, f32[2,768]{1,0:T(2...) custom-call(bf16[3,180,2,768]{3,2,1,0:T(2,128)(2,1)} %bitcast.4, bf16[3,180,2,768]{3,2,1,0:T(2,128)(2,1)} %bitcast.5, ...), custom_call_target="tpu_custom_call" | custom-call | tf_op jit(solution)/shard_map/mixer/pallas_call | solution.py:741
  114.3 2.3 %settle.1 = (bf16[3,180,2,768]{3,2,1,0:T(2,128)(2,1)}, bf16[3,180,2,768]{3,2,1,0:T(2,128)(2,1)}, f32[2,8,96,96]{3,2,1,0:T(8,128)}, f32[2,768]{1,0:T(2,128)}, f32[2,8,96,96]{3,2,1,0:T(8,128)}, /*index=5*/f32[2,768]{1,0:T(2,128)}) custom-call(bf16[3,180,2,768]{3,2,1,0:T(2,128)(2,1)S(1)} %get-tuple-element.18.refs_0_, ...), custom_call_target="tpu_custom_call" | custom-call | tf_op jit(solution)/shard_map/settle/pallas_call | solution.py:776

commit v5 on v4

--- a/solution.py
+++ b/solution.py
@@ -160,6 +160,7 @@
 MESH_ID = pl.DeviceIdType.MESH
 VMEM_LIMIT = 52 << 20
 FIRST, AFTER_E, AFTER_F = 2, 3, 2
+SPREAD = 11
 
 
 def host_tables(length, modes):
@@ -332,6 +333,7 @@
 
     def peer_at(j):
         peer = jnp.int32(0)
+        j = lax.rem(j * SPREAD, n)
         bit = 1
         while bit < n:
             peer = peer + bit * lax.rem(me // bit + j // bit, 2)
@@ -655,8 +657,7 @@
     for g in range(groups):
         for h in range(rows):
             move_c(g, h).left()
-    for h in range(rows - 1):
-        finish_d(last, h)
+    finish_d(last, 0)
     with jax.named_scope("swap2"):
         last_swap.wait()
     both[partner] = other[...].reshape(n * 16, channels)
@@ -672,7 +673,8 @@
                     block = dot(ordered, place, (1, 1))
                     for c in range(2):
                         out[c, g * PER_GROUP + i] = block[c * BLOCK : (c + 1) * BLOCK]
-    finish_d(last, rows - 1)
+    for h in range(1, rows):
+        finish_d(last, h)
     with jax.named_scope("end"):
         for g in range(groups):
             for h in range(rows):

time: 117 us -> 115 us (0.983)
    pallas_call x1, Pallas kernels: 114 us -> 112 us  [shards(): pl.pallas_call(functools.partial(mixer, n, inner, float(samples * reps)),...]
where the time goes in v5:
time: 115 us
  Pallas kernels  115 us (100%)
    pallas_call x1, Pallas kernels, shards(): pl.pallas_call(functools.partial(mixer, n, inner, float(samples * reps)),...  112 us

profile of v5, /device:TPU:0, one launch (start us, length us, event | category | flops | bytes accessed | tf_op | source)
XLA Modules:
  0.0 115.3 jit_solution(11975584638514479741)
XLA Ops:
  0.6 112.2 %mixer.1 = (bf16[3,180,2,768]{3,2,1,0:T(2,128)(2,1)S(1)}, bf16[3,180,2,768]{3,2,1,0:T(2,128)(2,1)S(1)}, f32[2,8,96,96]{3,2,1,0:T(8,128)S(1)}, f32[2,768]{1,0:T(2...) custom-call(bf16[3,180,2,768]{3,2,1,0:T(2,128)(2,1)} %bitcast.4, bf16[3,180,2,768]{3,2,1,0:T(2,128)(2,1)} %bitcast.5, ...), custom_call_target="tpu_custom_call" | custom-call | tf_op jit(solution)/shard_map/mixer/pallas_call | solution.py:743
  112.9 2.3 %settle.1 = (bf16[3,180,2,768]{3,2,1,0:T(2,128)(2,1)}, bf16[3,180,2,768]{3,2,1,0:T(2,128)(2,1)}, f32[2,8,96,96]{3,2,1,0:T(8,128)}, f32[2,768]{1,0:T(2,128)}, f32[2,8,96,96]{3,2,1,0:T(8,128)}, /*index=5*/f32[2,768]{1,0:T(2,128)}) custom-call(bf16[3,180,2,768]{3,2,1,0:T(2,128)(2,1)S(1)} %get-tuple-element.18.refs_0_, ...), custom_call_target="tpu_custom_call" | custom-call | tf_op jit(solution)/shard_map/settle/pallas_call | solution.py:778

commit v6 on v5

--- a/solution.py
+++ b/solution.py
@@ -161,6 +161,7 @@
 VMEM_LIMIT = 52 << 20
 FIRST, AFTER_E, AFTER_F = 2, 3, 2
 SPREAD = 11
+GREET = 9
 
 
 def host_tables(length, modes):
@@ -288,7 +289,7 @@
     barrier = pltpu.get_barrier_semaphore()
 
     def greet(j, carry):
-        peer = lax.rem(me + j, n)
+        peer = lax.rem(me + j * GREET, n)
         pl.semaphore_signal(barrier, inc=1, device_id={"seq": peer}, device_id_type=MESH_ID)
         return carry
 
@@ -673,12 +674,16 @@
                     block = dot(ordered, place, (1, 1))
                     for c in range(2):
                         out[c, g * PER_GROUP + i] = block[c * BLOCK : (c + 1) * BLOCK]
-    for h in range(1, rows):
+    for h in range(1, rows - 1):
         finish_d(last, h)
+    for g in range(last):
+        for h in range(rows):
+            move_d(g, h).left()
+    for h in range(rows - 1):
+        move_d(last, h).left()
+    finish_d(last, rows - 1)
     with jax.named_scope("end"):
-        for g in range(groups):
-            for h in range(rows):
-                move_d(g, h).left()
+        move_d(last, rows - 1).left()
 
 
 def settle(*refs):

time: 115 us -> 115 us (level)
  no operation moved by 1% of the time
where the time goes in v6:
time: 115 us
  Pallas kernels  114 us (99%)
    pallas_call x1, Pallas kernels, shards(): pl.pallas_call(functools.partial(mixer, n, inner, float(samples * reps)),...  112 us

profile of v6, /device:TPU:0, one launch (start us, length us, event | category | flops | bytes accessed | tf_op | source)
XLA Modules:
  0.0 115.2 jit_solution(995093636227983095)
XLA Ops:
  0.6 112.1 %mixer.1 = (bf16[3,180,2,768]{3,2,1,0:T(2,128)(2,1)S(1)}, bf16[3,180,2,768]{3,2,1,0:T(2,128)(2,1)S(1)}, f32[2,8,96,96]{3,2,1,0:T(8,128)S(1)}, f32[2,768]{1,0:T(2...) custom-call(bf16[3,180,2,768]{3,2,1,0:T(2,128)(2,1)} %bitcast.4, bf16[3,180,2,768]{3,2,1,0:T(2,128)(2,1)} %bitcast.5, ...), custom_call_target="tpu_custom_call" | custom-call | tf_op jit(solution)/shard_map/mixer/pallas_call | solution.py:748
  112.8 2.3 %settle.1 = (bf16[3,180,2,768]{3,2,1,0:T(2,128)(2,1)}, bf16[3,180,2,768]{3,2,1,0:T(2,128)(2,1)}, f32[2,8,96,96]{3,2,1,0:T(8,128)}, f32[2,768]{1,0:T(2,128)}, f32[2,8,96,96]{3,2,1,0:T(8,128)}, /*index=5*/f32[2,768]{1,0:T(2,128)}) custom-call(bf16[3,180,2,768]{3,2,1,0:T(2,128)(2,1)S(1)} %get-tuple-element.18.refs_0_, ...), custom_call_target="tpu_custom_call" | custom-call | tf_op jit(solution)/shard_map/settle/pallas_call | solution.py:783
